TPU v7x, 16 devices: a 4x2x1 block of a 4x4x8 slice. The times are simulated.
16 devices in a mesh: dp: 2 (over y, z), tp: 8 (over x, core).
Axes of the slice: x: 4, y: 2, z: 1, core: 2. Of those that a mesh axis runs over, the one named last changes fastest.
The devices are a block of a 4x4x8 slice.
Arguments:
- x_in: bfloat16 [512, 2048], P('dp'), parts along dimension 0
- lengths: int32 [512], P('dp'), parts along dimension 0
- k_cache: bfloat16 [2, 512, 256, 8, 128], P(None, 'dp', None, 'tp'), parts along dimension 1
- v_cache: bfloat16 [2, 512, 256, 8, 128], P(None, 'dp', None, 'tp'), parts along dimension 1
- g_attn: bfloat16 [2, 2048], replicated
- w_q: bfloat16 [2, 2048, 2048], P(None, None, 'tp')
- b_q: bfloat16 [2, 2048], P(None, 'tp')
- w_k: bfloat16 [2, 2048, 1024], P(None, None, 'tp')
- b_k: bfloat16 [2, 1024], P(None, 'tp')
- w_v: bfloat16 [2, 2048, 1024], P(None, None, 'tp')
- b_v: bfloat16 [2, 1024], P(None, 'tp')
- w_o: bfloat16 [2, 2048, 2048], P(None, 'tp')
- g_mlp: bfloat16 [2, 2048], replicated
- w_gate: bfloat16 [2, 2048, 11008], P(None, None, 'tp')
- w_up: bfloat16 [2, 2048, 11008], P(None, None, 'tp')
- w_down: bfloat16 [2, 11008, 2048], P(None, 'tp')
Outputs:
- output 1: bfloat16 [512, 2048], P('dp'), parts along dimension 0
- output 2: bfloat16 [2, 512, 8, 128], P(None, 'dp', 'tp'), parts along dimension 1
- output 3: bfloat16 [2, 512, 8, 128], P(None, 'dp', 'tp'), parts along dimension 1
There are 2 independent parts. A program takes and returns all parts, laid end to end along the dimension named above; an argument that names none is the same for every part.
All inputs are finite; a program needn't handle non-finite values.
Results may differ from a plain program's by a relative error of at most 0.0197908.
Values are sent between devices in bfloat16 or wider.
A program may use at most 768 MiB of HBM per device.

v0:
```python
import math
import jax
import jax.numpy as jnp
from jax import lax
from jax.sharding import PartitionSpec as P

EPS = 1e-6
THETA = 1000000.0


def rms_scale(x_float, gain_vec):
    mean_sq = jnp.mean(x_float * x_float, axis=-1, keepdims=True)
    return (x_float * lax.rsqrt(mean_sq + EPS) * gain_vec.astype(jnp.float32)).astype(jnp.bfloat16)


def rotary(vec_in, positions):
    half_dim = vec_in.shape[-1] // 2
    inv_freq = jnp.exp(jnp.arange(half_dim, dtype=jnp.float32) * (-2.0 * math.log(THETA) / vec_in.shape[-1]))
    angles = positions.astype(jnp.float32)[:, None, None] * inv_freq
    cos_part = jnp.cos(angles)
    sin_part = jnp.sin(angles)
    lo_half = vec_in[..., :half_dim]
    hi_half = vec_in[..., half_dim:]
    return jnp.concatenate([lo_half * cos_part - hi_half * sin_part, hi_half * cos_part + lo_half * sin_part], axis=-1)


def attend(q_rot, key_new, val_new, k_layer, v_layer, lengths):
    score_scale = q_rot.shape[-1] ** -0.5
    s_old = jnp.einsum('bsgh,btsh->bsgt', q_rot, k_layer, preferred_element_type=jnp.float32) * score_scale
    s_new = jnp.einsum('bsgh,bsh->bsg', q_rot, key_new, preferred_element_type=jnp.float32) * score_scale
    valid_mask = jnp.arange(k_layer.shape[1])[None, :] < lengths[:, None]
    s_old = jnp.where(valid_mask[:, None, None, :], s_old, -jnp.inf)
    row_max = jnp.maximum(jnp.max(s_old, axis=-1), s_new)
    w_old = jnp.exp(s_old - row_max[..., None])
    w_new = jnp.exp(s_new - row_max)
    weight_sum = jnp.sum(w_old, axis=-1) + w_new
    mixed_vals = jnp.einsum('bsgt,btsh->bsgh', w_old.astype(jnp.bfloat16), v_layer, preferred_element_type=jnp.float32)
    mixed_vals = mixed_vals + w_new[..., None] * val_new.astype(jnp.float32)[:, :, None, :]
    return (mixed_vals / weight_sum[..., None]).astype(jnp.bfloat16)


def decoder_layer(x_state, lengths, k_layer, v_layer, weights, combine):
    g_one, wq_one, bq_one, wk_one, bk_one, wv_one, bv_one, wo_one, g_two, wg_one, wu_one, wd_one = weights
    n_rows = x_state.shape[0]
    head_dim = k_layer.shape[-1]
    n_slots = k_layer.shape[-2]
    x_float = x_state.astype(jnp.float32)
    hidden = rms_scale(x_float, g_one)
    q_proj = (jnp.dot(hidden, wq_one, preferred_element_type=jnp.float32) + bq_one.astype(jnp.float32)).reshape(n_rows, -1, head_dim)
    k_proj = (jnp.dot(hidden, wk_one, preferred_element_type=jnp.float32) + bk_one.astype(jnp.float32)).reshape(n_rows, n_slots, head_dim)
    v_new = (jnp.dot(hidden, wv_one, preferred_element_type=jnp.float32) + bv_one.astype(jnp.float32)).reshape(n_rows, n_slots, head_dim).astype(jnp.bfloat16)
    q_rot = rotary(q_proj, lengths).astype(jnp.bfloat16).reshape(n_rows, n_slots, -1, head_dim)
    k_new = rotary(k_proj, lengths).astype(jnp.bfloat16)
    attn_rows = attend(q_rot, k_new, v_new, k_layer, v_layer, lengths).reshape(n_rows, -1)
    x_mid = (x_float + combine(jnp.dot(attn_rows, wo_one, preferred_element_type=jnp.float32))).astype(jnp.bfloat16)
    mid_float = x_mid.astype(jnp.float32)
    hidden_two = rms_scale(mid_float, g_two)
    gate_val = jnp.dot(hidden_two, wg_one, preferred_element_type=jnp.float32)
    up_val = jnp.dot(hidden_two, wu_one, preferred_element_type=jnp.float32)
    act_val = (jax.nn.silu(gate_val) * up_val).astype(jnp.bfloat16)
    x_next = (mid_float + combine(jnp.dot(act_val, wd_one, preferred_element_type=jnp.float32))).astype(jnp.bfloat16)
    return x_next, k_new, v_new


def tp_sum(part_sum):
    return lax.psum(part_sum.astype(jnp.bfloat16), 'tp').astype(jnp.float32)


def solution(mesh):
    cache_spec = P(None, 'dp', None, 'tp', None)
    col_spec = P(None, None, 'tp')
    row_spec = P(None, 'tp', None)
    vec_spec = P(None, 'tp')
    new_spec = P(None, 'dp', 'tp', None)
    in_specs = (P('dp', None), P('dp'), cache_spec, cache_spec, P(), col_spec, vec_spec, col_spec, vec_spec, col_spec, vec_spec, row_spec, P(), col_spec, col_spec, row_spec)
    out_specs = (P('dp', None), new_spec, new_spec)

    def local_step(x_in, lengths, k_cache, v_cache, g_attn, w_q, b_q, w_k, b_k, w_v, b_v, w_o, g_mlp, w_gate, w_up, w_down):
        x_state = x_in
        k_rows = []
        v_rows = []
        for layer_idx in range(k_cache.shape[0]):
            weights = tuple(stacked[layer_idx] for stacked in (g_attn, w_q, b_q, w_k, b_k, w_v, b_v, w_o, g_mlp, w_gate, w_up, w_down))
            x_state, k_new, v_new = decoder_layer(x_state, lengths, k_cache[layer_idx], v_cache[layer_idx], weights, tp_sum)
            k_rows.append(k_new)
            v_rows.append(v_new)
        return x_state, jnp.stack(k_rows), jnp.stack(v_rows)

    return jax.shard_map(local_step, mesh=mesh, in_specs=in_specs, out_specs=out_specs, check_vma=False)
```

profile of v0, /device:TPU:112, one launch (start us, length us, event | category | flops | bytes accessed | tf_op | source)
XLA Modules:
  0.0 337.7 jit_solution(17209049705082181988)
XLA Ops:
  7.3 0.7 convert_element_type.156
  7.9 0.8 iota_compare_fusion
  8.8 1.6 fusion.40
  10.4 1.3 bitcast_convert_fusion.1
  11.6 1.3 bitcast_convert_fusion
  13.0 1.3 slice_convert_fusion.4
  14.3 0.8 slice_convert_fusion.3
  15.1 0.5 multiply_cosine_fusion
  15.6 1.9 fusion.61
  17.6 0.3 fusion.117
  18.0 1.9 convolution_add_fusion.1
  20.6 0.4 pad_maximum_fusion
  21.0 0.4 fusion.139
  21.4 10.4 %fusion.135 = (f32[256,2]{1,0:T(8,128)S(1)}, f32[256,2,256]{2,1,0:T(2,128)S(1)}) fusion(bf16[256,2,128]{2,1,0:T(2,128)(2,1)S(1)} %pad_maximum_fusion, bf16[2,256,256,1,128]{4,2,1,3,0:T(8,128)(2,1)} %bitcast.189, pred[256,256]{1,0:T(8,128)(4,1)S(1)} %iota_compare_fusion), kind=kOutput, calls=%fused_computation.166 | convolution fusion | flops 33947136 | bytes 17500160 | tf_op jit(solution)/shard_map/bsgh,btsh->bsgt/dot_general | solution.py:29
  31.8 0.8 fusion.96
  32.6 1.8 fusion.136
  34.4 7.2 %fusion.77 = bf16[256,2,128]{2,1,0:T(2,128)(2,1)S(1)} fusion(bf16[2,256,256,1,128]{4,2,1,3,0:T(8,128)(2,1)} %bitcast.191, f32[256,2,256]{2,1,0:T(2,128)S(1)} %get-tuple-element.39, f32[256,2]{1,0:T(8,128)S(1)} %multiply_maximum_fusion.1, f32[256,2]{1,0:T(8,128)S(1)} %get-tuple-element.12, f32[256,128]{1,0:T(8,128)S(1)} %get-tuple-element.40, ...), kind=kOutput, calls=%fused_computation.89 | convolution fusion | flops 34078720 | bytes 17569792 | tf_op jit(solution)/shard_map/bsgt,btsh->bsgh/dot_general | solution.py:37
  41.7 1.4 convolution_convert_fusion.1
  43.4 0.6 slice_convert_fusion
  44.0 56.5 %all-reduce.5.cloned.1.call-done = bf16[256,2048]{1,0:T(8,128)(2,1)} async-done(((bf16[256,2048]{1,0:T(8,128)(2,1)}), bf16[256,2048]{1,0:T(8,128)(2,1)}) %all-reduce.5.cloned.1.call-update) | async-done | bytes 1048592 | tf_op jit(solution)/shard_map/psum | solution.py:66
  100.5 1.7 fusion.44
  102.3 4.3 %fusion.14 = f32[256,1376]{0,1:T(8,128)S(1)} fusion(bf16[2,2048,1376]{1,2,0:T(8,128)(2,1)} %param.29, bf16[256,2048]{1,0:T(8,128)(2,1)S(1)} %get-tuple-element.11, f32[2048]{0:T(1024)S(1)} %bitcast.185, f32[256]{0:T(256)S(1)} %add_rsqrt_fusion.2), kind=kOutput, calls=%fused_computation.18 | convolution fusion | flops 1444937728 | bytes 8102912 | tf_op jit(solution)/shard_map/dot_general | solution.py:58
  106.6 11.5 %fusion.34 = bf16[256,2048]{1,0:T(8,128)(2,1)} fusion(bf16[2,1376,2048]{2,1,0:T(8,128)(2,1)} %param.31, bf16[2,2048,1376]{1,2,0:T(8,128)(2,1)} %param.30, f32[256,1376]{0,1:T(8,128)S(1)} %fusion.14, bf16[256,2048]{1,0:T(8,128)(2,1)S(1)} %get-tuple-element.11, f32[2048]{0:T(1024)S(1)} %bitcast.186, f32[256]{0:T(256)S(1)} %add_rsqrt_fusion.2), kind=kOutput, calls=%fused_computation.44 | convolution fusion | flops 2890416128 | bytes 14787584 | tf_op jit(solution)/shard_map/dot_general | solution.py:61
  118.5 53.4 %all-reduce.7.cloned.1.call-done = bf16[256,2048]{1,0:T(8,128)(2,1)} async-done(((bf16[256,2048]{1,0:T(8,128)(2,1)}), bf16[256,2048]{1,0:T(8,128)(2,1)}) %all-reduce.7.cloned.1.call-update) | async-done | bytes 1048592 | tf_op jit(solution)/shard_map/psum | solution.py:66
  171.9 1.7 fusion.48
  173.7 0.5 fusion.50
  174.2 0.6 copy-done.4
  174.9 0.5 fusion.60
  175.4 0.3 fusion.121
  175.7 0.6 maximum_bitcast_fusion.1
  176.3 1.6 copy.29
  178.0 2.1 fusion.138
  180.1 1.8 convolution_add_fusion
  182.5 0.4 pad_maximum_fusion.1
  182.9 10.3 %fusion.137 = (f32[256,2]{1,0:T(8,128)S(1)}, f32[256,2,256]{2,1,0:T(2,128)S(1)}) fusion(bf16[256,2,128]{2,1,0:T(2,128)(2,1)S(1)} %pad_maximum_fusion.1, bf16[2,256,256,1,128]{4,2,1,3,0:T(8,128)(2,1)} %bitcast.190, pred[256,256]{1,0:T(8,128)(4,1)S(1)} %copy-done.10), kind=kOutput, calls=%fused_computation.168 | convolution fusion | flops 33947136 | bytes 17500160 | tf_op jit(solution)/shard_map/bsgh,btsh->bsgt/dot_general | solution.py:29
  193.2 0.4 fusion.140
  193.7 0.8 fusion.98
  194.5 7.2 %fusion.75 = bf16[256,2,128]{2,1,0:T(2,128)(2,1)S(1)} fusion(bf16[2,256,256,1,128]{4,2,1,3,0:T(8,128)(2,1)} %bitcast.192, f32[256,2,256]{2,1,0:T(2,128)S(1)} %get-tuple-element.43, f32[256,2]{1,0:T(8,128)S(1)} %multiply_maximum_fusion, f32[256,2]{1,0:T(8,128)S(1)} %get-tuple-element.8, f32[256,128]{1,0:T(8,128)S(1)} %copy-done.8, ...), kind=kOutput, calls=%fused_computation.87 | convolution fusion | flops 34078720 | bytes 17569792 | tf_op jit(solution)/shard_map/bsgt,btsh->bsgh/dot_general | solution.py:37
  201.8 1.4 convolution_convert_fusion
  203.2 0.3 all-reduce.11.cloned.1.call-start
  203.6 53.4 %all-reduce.9.cloned.1.call-done = bf16[256,2048]{1,0:T(8,128)(2,1)} async-done(((bf16[256,2048]{1,0:T(8,128)(2,1)}), bf16[256,2048]{1,0:T(8,128)(2,1)}) %all-reduce.9.cloned.1.call-update) | async-done | bytes 1048592 | tf_op jit(solution)/shard_map/psum | solution.py:66
  257.0 1.9 fusion.52
  258.9 4.3 %fusion.8 = f32[256,1376]{0,1:T(8,128)S(1)} fusion(bf16[2,2048,1376]{1,2,0:T(8,128)(2,1)} %param.29, bf16[256,2048]{1,0:T(8,128)(2,1)S(1)} %get-tuple-element.7, f32[2048]{0:T(1024)S(1)} %bitcast.180, f32[256]{0:T(256)S(1)} %add_rsqrt_fusion), kind=kOutput, calls=%fused_computation.12 | convolution fusion | flops 1444937728 | bytes 8102912 | tf_op jit(solution)/shard_map/dot_general | solution.py:58
  263.2 11.6 %fusion.37 = bf16[256,2048]{1,0:T(8,128)(2,1)} fusion(bf16[2,1376,2048]{2,1,0:T(8,128)(2,1)} %param.31, bf16[2,2048,1376]{1,2,0:T(8,128)(2,1)} %param.30, f32[256,1376]{0,1:T(8,128)S(1)} %fusion.8, bf16[256,2048]{1,0:T(8,128)(2,1)S(1)} %get-tuple-element.7, f32[2048]{0:T(1024)S(1)} %bitcast.181, f32[256]{0:T(256)S(1)} %add_rsqrt_fusion), kind=kOutput, calls=%fused_computation.45 | convolution fusion | flops 2890416128 | bytes 14787584 | tf_op jit(solution)/shard_map/dot_general | solution.py:61
  274.9 0.8 copy.26
  275.7 0.7 pad_maximum_fusion.2
  276.3 52.2 %all-reduce.11.cloned.1.call-done = bf16[256,2048]{1,0:T(8,128)(2,1)} async-done(((bf16[256,2048]{1,0:T(8,128)(2,1)}), bf16[256,2048]{1,0:T(8,128)(2,1)}) %all-reduce.11.cloned.1.call-update) | async-done | bytes 1048592 | tf_op jit(solution)/shard_map/psum | solution.py:66
  328.6 2.6 fusion.55
  (64 shorter events, 2.4 us)
Async XLA Ops:
  7.2 93.4 %all-reduce.5.cloned.1.call-start = ((), (), s32[]{:S(2)}) async-start(), calls=%async_computation | async-start | bytes 2097152 | tf_op jit(solution)/shard_map/psum | solution.py:66
  8.7 12.6 %copy-start.9 = (pred[256,256]{1,0:T(8,128)(4,1)}, pred[256,256]{1,0:T(8,128)(4,1)S(1)}, u32[]{:S(2)}) copy-start(pred[256,256]{1,0:T(8,128)(4,1)S(1)} %iota_compare_fusion) | copy-start | bytes 196612
  8.7 9.3 %copy-start.1 = (bf16[256,2048]{1,0:T(8,128)(2,1)S(1)}, bf16[256,2048]{1,0:T(8,128)(2,1)}, u32[]{:S(2)}) copy-start(bf16[256,2048]{1,0:T(8,128)(2,1)} %param.16) | copy-start | bytes 3145732
  10.4 9.6 %copy-start.17 = (f32[256]{0:T(256)}, f32[256]{0:T(256)S(1)}, u32[]{:S(2)}) copy-start(f32[256]{0:T(256)S(1)} %add_rsqrt_fusion.3) | copy-start | bytes 3076
  15.1 4.9 %copy-start.14 = (f32[1,2048]{1,0:T(1,128)}, f32[1,2048]{1,0:T(1,128)S(1)}, u32[]{:S(2)}) copy-start(f32[1,2048]{1,0:T(1,128)S(1)} %get-tuple-element.28) | copy-start | bytes 24580
  21.4 11.2 %copy-start.5 = (bf16[2,2048,128]{2,1,0:T(8,128)(2,1)S(1)}, bf16[2,2048,128]{2,1,0:T(8,128)(2,1)}, u32[]{:S(2)}) copy-start(bf16[2,2048,128]{2,1,0:T(8,128)(2,1)} %param.25) | copy-start | bytes 3145732
  34.4 7.2 %copy-start.2 = (bf16[2,256,2048]{2,1,0:T(8,128)(2,1)S(1)}, bf16[2,256,2048]{2,1,0:T(8,128)(2,1)}, u32[]{:S(2)}) copy-start(bf16[2,256,2048]{2,1,0:T(8,128)(2,1)} %param.27) | copy-start | bytes 6291460
  41.7 1.8 copy-start.12
  43.2 128.7 %all-reduce.7.cloned.1.call-start = ((), (), s32[]{:S(2)}) async-start(), calls=%async_computation.1 | async-start | bytes 2097152 | tf_op jit(solution)/shard_map/psum | solution.py:66
  118.2 138.8 %all-reduce.9.cloned.1.call-start = ((), (), s32[]{:S(2)}) async-start(), calls=%async_computation.2 | async-start | bytes 2097152 | tf_op jit(solution)/shard_map/psum | solution.py:66
  171.9 1.8 copy-start
  173.6 1.2 copy-start.4
  173.6 1.2 copy-start.15
  174.2 3.8 %copy-start.16 = (f32[128]{0:T(128)S(1)}, f32[128]{0:T(128)}, u32[]{:S(2)}) copy-start(f32[128]{0:T(128)} %get-tuple-element.34) | copy-start | bytes 1540
  174.2 5.9 %copy-start.18 = (f32[1,256]{1,0:T(1,128)S(1)}, f32[1,256]{1,0:T(1,128)}, u32[]{:S(2)}) copy-start(f32[1,256]{1,0:T(1,128)} %get-tuple-element.32) | copy-start | bytes 3076
  181.9 1.0 copy-start.10
  182.9 10.3 %copy-start.7 = (bf16[256,128,1]{1,2,0:T(2,128)(2,1)S(1)}, bf16[256,128,1]{1,2,0:T(2,128)(2,1)}, u32[]{:S(2)}) copy-start(bf16[256,128,1]{1,2,0:T(2,128)(2,1)} %copy.29) | copy-start | bytes 196612
  193.2 1.3 copy-start.8
  194.5 7.3 %copy-start.3 = (bf16[2,256,2048]{2,1,0:T(8,128)(2,1)S(1)}, bf16[2,256,2048]{2,1,0:T(8,128)(2,1)}, u32[]{:S(2)}) copy-start(bf16[2,256,2048]{2,1,0:T(8,128)(2,1)} %param.27) | copy-start | bytes 6291460
  203.2 55.6 %copy-start.13 = (f32[1,2048]{1,0:T(1,128)S(1)}, f32[1,2048]{1,0:T(1,128)}, u32[]{:S(2)}) copy-start(f32[1,2048]{1,0:T(1,128)} %get-tuple-element.26) | copy-start | bytes 24580
  203.2 125.3 %all-reduce.11.cloned.1.call-start = ((), (), s32[]{:S(2)}) async-start(), calls=%async_computation.3 | async-start | bytes 2097152 | tf_op jit(solution)/shard_map/psum | solution.py:66
  263.2 12.4 %copy-start.6 = (bf16[256,128]{1,0:T(8,128)(2,1)S(1)}, bf16[256,128]{1,0:T(8,128)(2,1)}, u32[]{:S(2)}) copy-start(bf16[256,128]{1,0:T(8,128)(2,1)} %get-tuple-element.45) | copy-start | bytes 196612
  263.2 12.4 %copy-start.11 = (bf16[256,128]{1,0:T(8,128)(2,1)S(1)}, bf16[256,128]{1,0:T(8,128)(2,1)}, u32[]{:S(2)}) copy-start(bf16[256,128]{1,0:T(8,128)(2,1)} %get-tuple-element.41) | copy-start | bytes 196612
Sparse Core Ops, SparseCore 0:
  43.3 57.2 all-reduce.4
  118.3 53.5 all-reduce.6
  203.3 53.5 all-reduce.8
  275.0 53.5 all-reduce.10
where the time goes:
time: 338 us
  waiting for transfers between devices  216 us (64%)
  matrix products  80.7 us (24%)
  other arithmetic  22.2 us (7%)
  between operations  14.3 us (4%)
  local copies, waits for them, and re-layouts  3.85 us (1%)
    psum x4, waiting for transfers between devices, tp_sum(): return lax.psum(part_sum.astype(jnp.bfloat16), 'tp').astype(jnp.float32)  216 us
    dot_general x2, matrix products, decoder_layer(): jnp.dot(act_val, wd_one, preferred_element_type=jnp.float32)  23.1 us
    dot_general x2, matrix products, attend(): jnp.einsum('bsgh,btsh->bsgt', q_rot, k_layer, preferred_element_type=jnp....  20.7 us
    dot_general x2, matrix products, attend(): jnp.einsum('bsgt,btsh->bsgh', w_old.astype(jnp.bfloat16), v_layer, prefer...  14.5 us
    dot_general x2, matrix products, decoder_layer(): gate_val = jnp.dot(hidden_two, wg_one, preferred_element_type=jnp.float32)  8.68 us
    reduce_sum x4, other arithmetic, rms_scale(): mean_sq = jnp.mean(x_float * x_float, axis=-1, keepdims=True)  6.93 us
  transfers between devices with their start and end apart: 4, of which 4 were waited for; matrix products, arithmetic and copies ran while one was open for 1% of the time, Pallas kernels for 0%

commit v1 on v0

v1 whole, which is shorter than its diff:
```python
import functools
import math
import jax
import jax.numpy as jnp
from jax import lax
from jax.experimental import pallas as pl
from jax.experimental.pallas import tpu as pltpu
from jax.sharding import PartitionSpec as P

EPS = 1e-6
THETA = 1000000.0
MESH = pl.DeviceIdType.MESH
F32 = jnp.float32
BF16 = jnp.bfloat16


def norm_rows(x, gain):
    mean_sq = jnp.mean(x * x, axis=-1, keepdims=True)
    return (x * lax.rsqrt(mean_sq + EPS) * gain).astype(BF16)


def pick(ref, idx):
    both = ref[...].astype(F32)
    return jnp.where(idx == 0, both[0:1], both[1:2])


def dot_nn(a, b):
    return jnp.dot(a, b, preferred_element_type=F32)


def dot_nt(a, b):
    return lax.dot_general(a, b, (((1,), (1,)), ((), ())), preferred_element_type=F32)


def kernel(layers, tp, x_hbm, len_ref, cos_ref, sin_ref, kc_hbm, vc_hbm, ga_ref, wq_hbm, bq_ref, wk_hbm, bk_ref,
           wv_hbm, bv_ref, wo_hbm, gm_ref, wg_hbm, wu_hbm, wd_hbm,
           xo_hbm, kn_hbm, vn_hbm,
           wq_v, wkv_v, wo_v, wg_v, wu_v, wd_v, k_v, v_v,
           part, hbuf, xres, r0, asum, s1, fin,
           qsend, qrecv, kbuf, vbuf, qrows, srows, orows, asend, arecv, act,
           wsem, kvsem, xsem, osem, ssem, rsem, qssem, qrsem):
    i = lax.axis_index("tp")
    chips = tp // 2
    x, c = i // 2, i % 2
    sib = 2 * x + 1 - c
    right = 2 * ((x + 1) % chips) + c
    left = 2 * ((x + chips - 1) % chips) + c
    xr, xl, xo = (x + 1) % chips, (x + chips - 1) % chips, (x + 2) % chips
    idr, idl, ido = 2 * xr + c, 2 * xl + c, 2 * xo + c
    base, m = (i // 4) * 4, i % 4
    cross = base + 3 - m
    width = wg_hbm.shape[1]
    n_seq = k_v.shape[0]

    def load(kind, l):
        copy = pltpu.make_async_copy
        if kind == "q":
            return [copy(wq_hbm.at[l], wq_v, wsem.at[0])]
        if kind == "kv":
            return [copy(wk_hbm.at[l], wkv_v.at[:, 0:128], wsem.at[1]),
                    copy(wv_hbm.at[l], wkv_v.at[:, 128:256], wsem.at[2])]
        if kind == "o":
            return [copy(wo_hbm.at[l], wo_v, wsem.at[3])]
        if kind == "gu":
            return [copy(wg_hbm.at[l], wg_v.at[pl.ds(0, width)], wsem.at[4]),
                    copy(wu_hbm.at[l], wu_v.at[pl.ds(0, width)], wsem.at[5])]
        if kind == "d":
            return [copy(wd_hbm.at[l], wd_v.at[pl.ds(0, width)], wsem.at[6])]
        if kind == "k":
            return [copy(kc_hbm.at[l, pl.ds(m * n_seq, n_seq)], k_v, kvsem.at[0])]
        return [copy(vc_hbm.at[l, pl.ds(m * n_seq, n_seq)], v_v, kvsem.at[1])]

    def start(kind, l):
        for cp in load(kind, l):
            cp.start()

    def wait(kind, l):
        for cp in load(kind, l):
            cp.wait()

    x_copy = pltpu.make_async_copy(x_hbm, part, xsem)
    x_copy.start()
    start("q", 0)
    start("kv", 0)
    start("k", 0)
    start("v", 0)

    barrier = pltpu.get_barrier_semaphore()
    for peer in (sib, right, left, cross):
        pl.semaphore_signal(barrier, inc=1, device_id={"tp": peer}, device_id_type=MESH)

    pad = wg_v.shape[0] - width
    wg_v[pl.ds(width, pad)] = jnp.zeros((pad, wg_v.shape[1]), BF16)
    wu_v[pl.ds(width, pad)] = jnp.zeros((pad, wu_v.shape[1]), BF16)
    wd_v[pl.ds(width, pad)] = jnp.zeros((pad, wd_v.shape[1]), BF16)

    x_copy.wait()
    gain0 = pick(ga_ref, 0)
    for j in range(tp):
        hbuf[j] = norm_rows(part[j // 2, j % 2].astype(F32), gain0)
    xres[...] = part[x, c]
    pl.semaphore_wait(barrier, 4)

    def remote(src, dst, k, dev):
        return pltpu.make_async_remote_copy(src_ref=src, dst_ref=dst, send_sem=ssem.at[k], recv_sem=rsem.at[k],
                                            device_id={"tp": dev}, device_id_type=MESH)

    def reduce_rows():
        order = (xo, xr, xl, x)
        d2d = [remote(part.at[q, 1 - c], r0.at[q], n, sib) for n, q in enumerate(order)]
        for cp in d2d:
            cp.start()
        lo, hi = pl.ds(0, 16), pl.ds(16, 16)

        def chip_sum(n):
            d2d[n].wait_recv()
            return part[order[n], c].astype(F32) + r0[order[n]].astype(F32)

        asum[0] = chip_sum(0).astype(BF16)
        s1r = remote(asum.at[0, lo], s1.at[0], 4, right)
        s1l = remote(asum.at[0, hi], s1.at[1], 5, left)
        s1r.start()
        s1l.start()
        to_right = chip_sum(1)
        asum[1, hi] = to_right[16:32].astype(BF16)
        s2r = remote(asum.at[1, hi], fin.at[0, hi], 6, right)
        s2r.start()
        to_left = chip_sum(2)
        asum[2, lo] = to_left[0:16].astype(BF16)
        s2l = remote(asum.at[2, lo], fin.at[1, lo], 7, left)
        s2l.start()
        s1r.wait_recv()
        asum[1, lo] = (part[xr, c, lo].astype(F32) + r0[xr, lo].astype(F32) + s1[0].astype(F32)).astype(BF16)
        s3r = remote(asum.at[1, lo], fin.at[0, lo], 8, right)
        s3r.start()
        s1l.wait_recv()
        asum[2, hi] = (part[xl, c, hi].astype(F32) + r0[xl, hi].astype(F32) + s1[1].astype(F32)).astype(BF16)
        s3l = remote(asum.at[2, hi], fin.at[1, hi], 9, left)
        s3l.start()
        own = chip_sum(3)
        for cp in (s2r, s2l, s3r, s3l):
            cp.wait_recv()
        total = own + fin[0].astype(F32) + fin[1].astype(F32)
        for cp in d2d + [s1r, s1l, s2r, s2l, s3r, s3l]:
            cp.wait_send()
        return total + xres[...].astype(F32)

    def gather_rows():
        lo, hi = pl.ds(0, 16), pl.ds(16, 16)
        own_r0 = remote(hbuf.at[i, lo], hbuf.at[i, lo], 10, right)
        own_l0 = remote(hbuf.at[i, hi], hbuf.at[i, hi], 11, left)
        own_r1 = remote(hbuf.at[i, hi], hbuf.at[i, hi], 12, right)
        own_l1 = remote(hbuf.at[i, lo], hbuf.at[i, lo], 13, left)
        own_s = remote(hbuf.at[i], hbuf.at[i], 16, sib)
        for cp in (own_r0, own_l0, own_r1, own_l1, own_s):
            cp.start()
        own_r0.wait_recv()
        fwd_r = remote(hbuf.at[idl, lo], hbuf.at[idl, lo], 14, right)
        fwd_r.start()
        own_l0.wait_recv()
        fwd_l = remote(hbuf.at[idr, hi], hbuf.at[idr, hi], 15, left)
        fwd_l.start()
        own_r1.wait_recv()
        sib_l = remote(hbuf.at[idl], hbuf.at[idl], 17, sib)
        sib_l.start()
        own_l1.wait_recv()
        sib_r = remote(hbuf.at[idr], hbuf.at[idr], 18, sib)
        sib_r.start()
        fwd_r.wait_recv()
        sib_o0 = remote(hbuf.at[ido, lo], hbuf.at[ido, lo], 19, sib)
        sib_o0.start()
        fwd_l.wait_recv()
        sib_o1 = remote(hbuf.at[ido, hi], hbuf.at[ido, hi], 20, sib)
        sib_o1.start()
        for cp in (own_s, sib_l, sib_r, sib_o0, sib_o1):
            cp.wait_recv()
        for cp in (own_r0, own_l0, own_r1, own_l1, own_s, fwd_r, fwd_l, sib_l, sib_r, sib_o0, sib_o1):
            cp.wait_send()

    def swap(src, dst, n0):
        copies = []
        for d in (1, 2, 3):
            to = (m + d) % 4
            cp = pltpu.make_async_remote_copy(src_ref=src.at[to], dst_ref=dst.at[m], send_sem=qssem.at[n0 + d - 1],
                                              recv_sem=qrsem.at[n0 + d - 1], device_id={"tp": base + to},
                                              device_id_type=MESH)
            cp.start()
            copies.append(cp)
        dst[m] = src[m]
        return copies

    def turn(v):
        return v * cos_ref[...] + pltpu.roll(v, 64, 1) * sin_ref[...]

    scale = 128.0 ** -0.5

    def layer(l, carry):
        more = l + 1 < layers
        h = hbuf[...].reshape(tp * hbuf.shape[1], hbuf.shape[2])
        wait("q", l)
        wait("kv", l)
        q = dot_nn(h, wq_v[...]) + pick(bq_ref, l)
        for j in range(2):
            qsend[:, :, 128 * j:128 * j + 128] = turn(q[:, 128 * j:128 * j + 128]).astype(BF16).reshape(4, n_seq, 128)
        q_copies = swap(qsend, qrecv, 0)
        kv = dot_nn(h, wkv_v[...])
        kbuf[...] = turn(kv[:, 0:128] + pick(bk_ref, l)).astype(BF16).reshape(4, n_seq, 128)
        vbuf[...] = (kv[:, 128:256] + pick(bv_ref, l)).astype(BF16).reshape(4, n_seq, 128)
        kv_out = [pltpu.make_async_copy(kbuf, kn_hbm.at[l], osem.at[0]),
                  pltpu.make_async_copy(vbuf, vn_hbm.at[l], osem.at[1])]
        for cp in kv_out:
            cp.start()

        @pl.when(more)
        def _():
            start("q", l + 1)
            start("kv", l + 1)

        @pl.when(l == 0)
        def _():
            start("o", l)
            start("gu", l)
            start("d", l)

        for cp in q_copies:
            cp.wait_recv()
        for j in range(8):
            qrows[pl.ds(j, n_seq, stride=8), :] = qrecv[j // 2, :, 128 * (j % 2):128 * (j % 2) + 128].astype(F32)
        wait("k", l)

        def scores(step, carry):
            for u in range(8):
                b = step * 8 + u
                rows = pl.ds(pl.multiple_of(b * 8, 8), 8)
                s = dot_nt(qrows[rows].astype(BF16), k_v[b]) * scale
                t = lax.broadcasted_iota(jnp.int32, s.shape, 1)
                srows[rows] = jnp.where(t < len_ref[m * n_seq + b], s, -jnp.inf)
            return carry

        lax.fori_loop(0, n_seq // 8, scores, 0)
        wait("v", l)

        def mix(step, carry):
            rows = pl.ds(pl.multiple_of(step * 128, 128), 128)
            seqs = pl.ds(pl.multiple_of(step * 16, 16), 16)
            s = srows[rows]
            k16 = jnp.broadcast_to(kbuf[m, seqs].astype(F32)[:, None, :], (16, 8, 128)).reshape(128, 128)
            v16 = jnp.broadcast_to(vbuf[m, seqs].astype(F32)[:, None, :], (16, 8, 128)).reshape(128, 128)
            s_new = jnp.sum(qrows[rows] * k16, axis=-1, keepdims=True) * scale
            top = jnp.maximum(jnp.max(s, axis=-1, keepdims=True), s_new)
            w = jnp.exp(s - top)
            w_new = jnp.exp(s_new - top)
            den = jnp.sum(w, axis=-1, keepdims=True) + w_new
            mixed = jnp.concatenate(
                [dot_nn(w[8 * u:8 * u + 8].astype(BF16), v_v[step * 16 + u]) for u in range(16)], axis=0)
            orows[rows] = (mixed + w_new * v16) / den
            return carry

        lax.fori_loop(0, n_seq // 16, mix, 0)

        @pl.when(more)
        def _():
            start("k", l + 1)
            start("v", l + 1)

        for cp in q_copies:
            cp.wait_send()
        for j in range(8):
            asend[j // 2, :, 128 * (j % 2):128 * (j % 2) + 128] = orows[pl.ds(j, n_seq, stride=8), :].astype(BF16)
        a_copies = swap(asend, arecv, 3)
        wait("o", l)
        for cp in a_copies:
            cp.wait_recv()
        a = arecv[...].reshape(4 * n_seq, 256)
        for j in range(4):
            cols = slice(512 * j, 512 * j + 512)
            part[:, :, :, cols] = dot_nn(a, wo_v[:, cols]).astype(BF16).reshape(part.shape[:3] + (512,))

        @pl.when(more)
        def _():
            start("o", l + 1)

        x_mid = reduce_rows().astype(BF16)
        for cp in a_copies:
            cp.wait_send()
        for cp in kv_out:
            cp.wait()
        xres[...] = x_mid
        hbuf[i] = norm_rows(x_mid.astype(F32), pick(gm_ref, l))
        gather_rows()

        h = hbuf[...].reshape(tp * hbuf.shape[1], hbuf.shape[2])
        wait("gu", l)
        n_act = act.shape[1]
        for lo in range(0, n_act, 256):
            hi = min(lo + 256, n_act)
            gate = dot_nt(h, wg_v[lo:hi])
            up = dot_nt(h, wu_v[lo:hi])
            act[:, lo:hi] = (gate * jax.nn.sigmoid(gate) * up).astype(BF16)

        @pl.when(more)
        def _():
            start("gu", l + 1)

        wait("d", l)
        for j in range(8):
            cols = slice(256 * j, 256 * j + 256)
            part[:, :, :, cols] = dot_nn(act[...], wd_v[:, cols]).astype(BF16).reshape(part.shape[:3] + (256,))

        @pl.when(more)
        def _():
            start("d", l + 1)

        x_next = reduce_rows().astype(BF16)
        xres[...] = x_next
        normed = norm_rows(x_next.astype(F32), pick(ga_ref, jnp.minimum(l + 1, layers - 1)))
        hbuf[i] = jnp.where(more, normed.astype(F32), x_next.astype(F32)).astype(BF16)
        gather_rows()
        return carry

    lax.fori_loop(0, layers, layer, 0)
    out = pltpu.make_async_copy(hbuf, xo_hbm, xsem)
    out.start()
    out.wait()


def solution(mesh):
    cache_spec = P(None, 'dp', None, 'tp', None)
    col_spec = P(None, None, 'tp')
    row_spec = P(None, 'tp', None)
    vec_spec = P(None, 'tp')
    new_spec = P(None, 'dp', 'tp', None)
    in_specs = (P('dp', None), P('dp'), cache_spec, cache_spec, P(), col_spec, vec_spec, col_spec, vec_spec, col_spec, vec_spec, row_spec, P(), col_spec, col_spec, row_spec)
    out_specs = (P('dp', None), new_spec, new_spec)
    tp = mesh.shape['tp']

    def local_step(x_in, lengths, k_cache, v_cache, g_attn, w_q, b_q, w_k, b_k, w_v, b_v, w_o, g_mlp, w_gate, w_up, w_down):
        layers, rows, t_len, _, dim = k_cache.shape
        d_model = x_in.shape[1]
        own, n_seq = rows // tp, rows // 4
        half = dim // 2
        width = w_down.shape[1]
        wide = -(-width // 128) * 128
        inv_freq = jnp.exp(jnp.arange(half, dtype=F32) * (-2.0 * math.log(THETA) / dim))
        angles = lengths.astype(F32)[:, None] * inv_freq
        cos, sin = jnp.cos(angles), jnp.sin(angles)
        cos2 = jnp.concatenate([cos, cos], axis=-1)
        sin2 = jnp.concatenate([-sin, sin], axis=-1)
        any_spec = pl.BlockSpec(memory_space=pl.ANY)
        vmem = pl.BlockSpec(memory_space=pltpu.VMEM)
        smem = pl.BlockSpec(memory_space=pltpu.SMEM)
        x_out, k_new, v_new = pl.pallas_call(
            functools.partial(kernel, layers, tp),
            name="decode",
            out_shape=(jax.ShapeDtypeStruct((tp, own, d_model), BF16),
                       jax.ShapeDtypeStruct((layers, 4, n_seq, dim), BF16),
                       jax.ShapeDtypeStruct((layers, 4, n_seq, dim), BF16)),
            in_specs=[any_spec, smem, vmem, vmem, any_spec, any_spec, vmem, any_spec, vmem, any_spec, vmem,
                      any_spec, vmem, any_spec, vmem, any_spec, any_spec, any_spec],
            out_specs=(any_spec, any_spec, any_spec),
            scratch_shapes=[
                pltpu.VMEM((d_model, 256), BF16),
                pltpu.VMEM((d_model, 256), BF16),
                pltpu.VMEM((256, d_model), BF16),
                pltpu.VMEM((wide, d_model), BF16),
                pltpu.VMEM((wide, d_model), BF16),
                pltpu.VMEM((wide, d_model), BF16),
                pltpu.VMEM((n_seq, t_len, dim), BF16),
                pltpu.VMEM((n_seq, t_len, dim), BF16),
                pltpu.VMEM((tp // 2, 2, own, d_model), BF16),
                pltpu.VMEM((tp, own, d_model), BF16),
                pltpu.VMEM((own, d_model), BF16),
                pltpu.VMEM((tp // 2, own, d_model), BF16),
                pltpu.VMEM((3, own, d_model), BF16),
                pltpu.VMEM((2, own // 2, d_model), BF16),
                pltpu.VMEM((2, own, d_model), BF16),
                pltpu.VMEM((4, n_seq, 256), BF16),
                pltpu.VMEM((4, n_seq, 256), BF16),
                pltpu.VMEM((4, n_seq, dim), BF16),
                pltpu.VMEM((4, n_seq, dim), BF16),
                pltpu.VMEM((n_seq * 8, dim), F32),
                pltpu.VMEM((n_seq * 8, t_len), F32),
                pltpu.VMEM((n_seq * 8, dim), F32),
                pltpu.VMEM((4, n_seq, 256), BF16),
                pltpu.VMEM((4, n_seq, 256), BF16),
                pltpu.VMEM((rows, wide), BF16),
                pltpu.SemaphoreType.DMA((7,)),
                pltpu.SemaphoreType.DMA((2,)),
                pltpu.SemaphoreType.DMA,
                pltpu.SemaphoreType.DMA((2,)),
                pltpu.SemaphoreType.DMA((21,)),
                pltpu.SemaphoreType.DMA((21,)),
                pltpu.SemaphoreType.DMA((6,)),
                pltpu.SemaphoreType.DMA((6,)),
            ],
            compiler_params=pltpu.CompilerParams(collective_id=0, has_side_effects=True, vmem_limit_bytes=60 * 1024 * 1024),
        )(x_in.reshape(tp // 2, 2, own, d_model), lengths, cos2, sin2,
          k_cache.reshape(layers, rows, t_len, dim), v_cache.reshape(layers, rows, t_len, dim),
          g_attn, w_q, b_q, w_k, b_k, w_v, b_v, w_o, g_mlp,
          w_gate.transpose(0, 2, 1), w_up.transpose(0, 2, 1), w_down)
        return (x_out.reshape(rows, d_model), k_new.reshape(layers, rows, 1, dim), v_new.reshape(layers, rows, 1, dim))

    return jax.shard_map(local_step, mesh=mesh, in_specs=in_specs, out_specs=out_specs, check_vma=False)
```

time: 338 us -> 122 us (0.36)
  waiting for transfers between devices: 216 us -> 0 us
  Pallas kernels: 0 us -> 113 us
  matrix products: 80.7 us -> 0 us
  other arithmetic: 22.2 us -> 2.07 us
  between operations: 14.3 us -> 0.65 us
    psum x4 -> x0, waiting for transfers between devices: 216 us -> none  [tp_sum(): return lax.psum(part_sum.astype(jnp.bfloat16), 'tp').astype(jnp.float32)]
    pallas_call x0 -> x1, Pallas kernels: none -> 113 us  [local_step(): pl.pallas_call(functools.partial(kernel, layers, tp), name='decode', out_...]
    dot_general x18 -> x0, matrix products: 80.7 us -> none  [the longest x2 23.1 us: decoder_layer(): jnp.dot(act_val, wd_one, preferred_element_type=jnp.float32)]
    reduce_sum x6 -> x0, other arithmetic: 8.43 us -> none  [the longest x4 6.93 us: rms_scale(): mean_sq = jnp.mean(x_float * x_float, axis=-1, keepdims=True)]
    add x5 -> x0, other arithmetic: 3.98 us -> none  [the longest x1 1.32 us: decoder_layer(): jnp.dot(hidden, wq_one, preferred_element_type=jnp.float32)]
  transfers between devices with their start and end apart: 4 -> 0, of which waited for: 4 -> 0; matrix products, arithmetic and copies ran while one was open for 1% -> 0% of each run, Pallas kernels for 0% -> 0%
where the time goes in v1:
time: 122 us; the launch traced here: 121 us
  Pallas kernels  113 us (93%)
  local copies, waits for them, and re-layouts  5.44 us (4%)
  other arithmetic  2.07 us (2%)
    pallas_call x1, Pallas kernels, local_step(): pl.pallas_call(functools.partial(kernel, layers, tp), name='decode', out_...  113 us
    unnamed x3, local copies, waits for them, and re-layouts  5.44 us

profile of v1, /device:TPU:112, one launch (start us, length us, event | category | flops | bytes accessed | tf_op | source)
XLA Modules:
  0.0 120.8 jit_solution(8624741921893584631)
XLA Ops:
  0.6 0.7 convert_element_type.3
  1.3 0.5 fusion
  1.9 0.8 pad_maximum_fusion
  2.7 112.6 %decode.1 = (bf16[8,32,2048]{2,1,0:T(8,128)(2,1)}, bf16[2,4,64,128]{3,2,1,0:T(8,128)(2,1)}, bf16[2,4,64,128]{3,2,1,0:T(8,128)(2,1)}) custom-call(bf16[4,2,32,2048]{3,2,1,0:T(8,128)(2,1)} %bitcast.16, s32[256]{0:T(256)} %len_ref.1, f32[256,128]{1,0:T(8,128)} %get-tuple-element.15.cos_ref, f32[256,128]{1,0:T(8,128)} %get-tuple-element.16.sin_ref, ...), custom_call_target="tpu_custom_call" | custom-call | tf_op jit(solution)/shard_map/decode/pallas_call | solution.py:352
  115.3 2.3 %copy.24 = bf16[256,2048]{1,0:T(8,128)(2,1)} copy(bf16[256,2048]{1,0:T(8,128)(2,1)} %bitcast.17) | data formatting | bytes 2097152
  117.6 1.6 %copy.25 = bf16[2,256,1,128]{3,1,2,0:T(8,128)(2,1)} copy(bf16[2,256,1,128]{3,1,2,0:T(8,128)(2,1)} %bitcast.19) | data formatting | bytes 262144
  119.2 1.6 %copy.26 = bf16[2,256,1,128]{3,1,2,0:T(8,128)(2,1)} copy(bf16[2,256,1,128]{3,1,2,0:T(8,128)(2,1)} %bitcast.18) | data formatting | bytes 262144
  (1 shorter events, 0.0 us)
